TPU v7x, 128 devices: a whole 4x4x4 slice. The times are simulated.
128 devices in a mesh: fsdp: 32 (over y, z_lo, x), tp: 4 (over z_hi, core).
Axes of the slice: x: 4, y: 4, z: 4 (z_hi: 2, z_lo: 2; z = z_hi * 2 + z_lo), core: 2. Of those that a mesh axis runs over, the one named last changes fastest.
Arguments:
- partials: bfloat16 [32, 2, 5120, 1024], P('fsdp', None, None, 'tp'), may hold values from -6 to 6
- token_counts: int32 [32], P('fsdp'), may hold values from 100 to 599
- owner_map: int32 [2, 4], replicated, may hold values from 0 to 3, each once within a row
- params: float32 [2, 5120, 1024], P(None, 'fsdp', 'tp'), may hold values from -0.75 to 0.75
- moment1: float32 [2, 5120, 1024], P(None, 'fsdp', 'tp'), may hold values from -0.15625 to 0.15625
- moment2: float32 [2, 5120, 1024], P(None, 'fsdp', 'tp'), may hold values from 0.0001 to 0.004
Outputs:
- new_params: float32 [2, 5120, 1024], P(None, 'fsdp', 'tp')
- new_moment1: float32 [2, 5120, 1024], P(None, 'fsdp', 'tp')
- new_moment2: float32 [2, 5120, 1024], P(None, 'fsdp', 'tp')
- rollout_delta: bfloat16 [2, 5120, 1024], P(None, None, 'tp')
Inputs may be any that keep to these rules, and one draw needn't show every extreme that they name: `owner_map`: each row is a permutation of 0 to 3.
All inputs are finite; a program needn't handle non-finite values.
Results may differ from a plain program's by a relative error of at most 0.0004.
Values may be sent and summed in bfloat16 or wider, within the bound.
A program may use at most 64 MiB of HBM per device.

v0:
```python
import jax
import jax.numpy as jnp
from jax import lax
from jax.sharding import Mesh
from jax.sharding import PartitionSpec as P

STEP = 10
FSDP = ("fsdp_0", "fsdp_1", "fsdp_2")


def sent_to_all(value, axis):
    peers = lax.axis_size(axis)
    return lax.all_to_all(
        jnp.broadcast_to(value[None], (peers, *value.shape)), axis, 0, 0, tiled=True
    )


def over_copies(value, axis):
    everything = sent_to_all(value, axis)
    return jnp.sum(everything, axis=0)


def joined_along(tiles, dim):
    tiles = jnp.moveaxis(tiles, 0, dim)
    dims = tiles.shape
    return tiles.reshape(*dims[:dim], dims[dim] * dims[dim + 1], *dims[dim + 2 :])


def collect(value, axis, dim):
    return joined_along(sent_to_all(value, axis), dim)


def all_blocks(value, axes, order):
    tiles = value[None]
    for k in order:
        tiles = lax.all_gather(tiles, axes[k], axis=0, tiled=True)
    carried = [lax.axis_size(axes[k]) for k in reversed(order)]
    tiles = tiles.reshape(*carried, *value.shape)
    turned = sorted(range(len(order)), key=lambda place: order[len(order) - 1 - place])
    return tiles.transpose(*turned, *range(len(order), tiles.ndim)).reshape(-1, *value.shape)


def whole_of(value, axes, order, dim):
    return joined_along(all_blocks(value, axes, order), dim)


def local(partials, token_counts, owner_map, params, moment1, moment2):
    weight = token_counts.astype(jnp.float32)[0]
    total = over_copies(weight, FSDP)
    counts = collect(token_counts, FSDP, 0).astype(jnp.float32)
    arrived = lax.all_to_all(partials, FSDP, split_axis=2, concat_axis=0, tiled=True)
    summed = jnp.sum(counts[:, None, None, None] * arrived.astype(jnp.float32), axis=0)
    grad = summed / total
    first = 0.9 * moment1 + 0.1 * grad
    second = 0.999 * moment2 + 0.001 * grad * grad
    bias_one = 1.0 - 0.9**STEP
    bias_two = 1.0 - 0.999**STEP
    direction = first / bias_one / (jnp.sqrt(second / bias_two) + 1e-08)
    new_params = params - 0.001 * (direction + 0.1 * params)
    delta = direction.astype(jnp.bfloat16)
    owners = lax.axis_size("tp")
    column = lax.axis_index("tp")
    served = lax.dynamic_index_in_dim(owner_map, column, 1, keepdims=False)
    select = served[:, None] == jnp.arange(owners, dtype=jnp.int32)[None, :]
    wide = collect(delta, "tp", 2)
    block = wide.shape[2] // owners
    split = wide.reshape(wide.shape[0], wide.shape[1], owners, block)
    kept = jnp.where(select[:, None, :, None], split, jnp.zeros((), jnp.bfloat16))
    rollout = whole_of(jnp.sum(kept, axis=2), FSDP, (1, 0, 2), 1)
    return (new_params, first, second, rollout)


def solution(mesh):
    split = Mesh(
        mesh.devices.reshape(4, 2, 4, mesh.shape["tp"]), ("fsdp_0", "fsdp_1", "fsdp_2", "tp")
    )
    return jax.shard_map(
        local,
        mesh=split,
        in_specs=(
            P(FSDP, None, None, "tp"),
            P(FSDP),
            P(),
            P(None, FSDP, "tp"),
            P(None, FSDP, "tp"),
            P(None, FSDP, "tp"),
        ),
        out_specs=(
            P(None, FSDP, "tp"),
            P(None, FSDP, "tp"),
            P(None, FSDP, "tp"),
            P(None, None, "tp"),
        ),
        check_vma=False,
    )
```

profile of v0, /device:TPU:1, one launch (start us, length us, event | category | flops | bytes accessed | tf_op | source)
XLA Modules:
  0.0 245.0 jit_solution(1411335727446816097)
XLA Ops:
  7.2 0.0 copy-start
  7.8 0.6 broadcast_in_dim.41
  8.5 9.2 %all-to-all-start = ((s32[32,1,1]{2,1,0:T(1,128)}), s32[32,1,1]{2,1,0:T(1,128)S(1)}, u32[]{:S(2)}, u32[]{:S(2)}) async-start(s32[32,1,1]{2,1,0:T(1,128)} %broadcast_in_dim.41), calls=%async_computation | async-start | bytes 32768 | tf_op jit(solution)/shard_map/all_to_all | solution.py:13
  17.7 7.1 %all-to-all-done = s32[32,1,1]{2,1,0:T(1,128)S(1)} async-done(((s32[32,1,1]{2,1,0:T(1,128)}), s32[32,1,1]{2,1,0:T(1,128)S(1)}, u32[]{:S(2)}, u32[]{:S(2)}) %all-to-all-start) | async-done | bytes 160 | tf_op jit(solution)/shard_map/all_to_all | solution.py:13
  24.8 0.6 broadcast_in_dim.43
  25.4 3.8 %all-to-all-start.2 = ((f32[32,1,1]{2,1,0:T(1,128)}), f32[32,1,1]{2,1,0:T(1,128)S(1)}, u32[]{:S(2)}, u32[]{:S(2)}) async-start(f32[32,1,1]{2,1,0:T(1,128)} %broadcast_in_dim.43), calls=%async_computation.2 | async-start | bytes 32768 | tf_op jit(solution)/shard_map/all_to_all | solution.py:13
  29.2 10.8 %copy.53 = bf16[1,2,5120,256]{3,1,0,2:T(2,128)(2,1)} copy(bf16[1,2,5120,256]{3,2,1,0:T(8,128)(2,1)} %param.6) | data formatting | bytes 10485760 | tf_op args[0]
  40.1 0.0 all-to-all-done.2
  40.1 7.8 %all-to-all-start.1 = ((bf16[1,2,5120,256]{3,1,0,2:T(2,128)(2,1)}), bf16[1,2,5120,256]{3,1,0,2:T(2,128)(2,1)}, u32[]{:S(2)}, u32[]{:S(2)}) async-start(bf16[1,2,5120,256]{3,1,0,2:T(2,128)(2,1)} %copy.53), calls=%async_computation.1 | async-start | bytes 10485760 | tf_op jit(solution)/shard_map/all_to_all | solution.py:51
  47.9 0.0 copy-start.4
  47.9 0.0 copy-start.5
  47.9 0.6 reduce_sum.31
  48.6 0.3 convert_reduce_fusion
  48.9 62.3 %all-to-all-done.1 = bf16[1,2,5120,256]{3,1,0,2:T(2,128)(2,1)} async-done(((bf16[1,2,5120,256]{3,1,0,2:T(2,128)(2,1)}), bf16[1,2,5120,256]{3,1,0,2:T(2,128)(2,1)}, u32[]{:S(2)}, u32[]{:S(2)}) %all-to-all-start.1) | async-done | bytes 5242912 | tf_op jit(solution)/shard_map/all_to_all | solution.py:51
  111.2 8.3 %fusion = f32[2,160,256]{2,0,1:T(2,128)S(1)} fusion(bf16[1,2,32,160,256]{4,1,3,2,0:T(2,128)(2,1)} %bitcast.12, f32[32]{0:T(128)S(1)} %convert_reduce_fusion), kind=kLoop, calls=%fused_computation.1 | loop fusion | flops 7782400 | bytes 5570688 | tf_op jit(solution)/shard_map/reduce_sum | solution.py:52
  119.5 0.9 fusion.3
  120.3 0.0 copy-start.1
  120.4 0.0 copy-start.2
  120.4 1.0 broadcast_in_dim.45
  121.4 6.2 %all-to-all-start.3 = ((bf16[4,2,160,256]{3,2,1,0:T(8,128)(2,1)}), bf16[4,2,160,256]{3,2,1,0:T(8,128)(2,1)S(1)}, u32[]{:S(2)}, u32[]{:S(2)}) async-start(bf16[4,2,160,256]{3,2,1,0:T(8,128)(2,1)} %broadcast_in_dim.45), calls=%async_computation.3 | async-start | bytes 1310720 | tf_op jit(solution)/shard_map/all_to_all | solution.py:13
  127.6 0.2 dynamic-slice_reduce_fusion
  127.8 10.6 %all-to-all-done.3 = bf16[4,2,160,256]{3,2,1,0:T(8,128)(2,1)S(1)} async-done(((bf16[4,2,160,256]{3,2,1,0:T(8,128)(2,1)}), bf16[4,2,160,256]{3,2,1,0:T(8,128)(2,1)S(1)}, u32[]{:S(2)}, u32[]{:S(2)}) %all-to-all-start.3) | async-done | bytes 655392 | tf_op jit(solution)/shard_map/all_to_all | solution.py:13
  138.3 0.1 fusion.1
  138.5 5.6 %all-gather = bf16[4,160,256]{2,1,0:T(8,128)(2,1)} all-gather(bf16[2,160,256]{2,1,0:T(8,128)(2,1)S(1)} %fusion.1), channel_id=2, replica_groups=mesh['fsdp_0'=4,'fsdp_1'=2,'fsdp_2'=4,'tp'=4] {'fsdp_1'}, dimensions={0}, use_global_device_ids=true | all-gather | bytes 491520 | tf_op jit(solution)/shard_map/all_gather | solution.py:36
  144.0 0.0 all-gather.4.cloned.1.call-update
  144.1 0.0 all-gather.6.cloned.1.call-start
  144.1 28.3 %all-gather.4.cloned.1.call-done = bf16[8,2,160,256]{3,2,1,0:T(8,128)(2,1)} async-done(((bf16[2,2,160,256]{3,2,1,0:T(8,128)(2,1)}), bf16[8,2,160,256]{3,2,1,0:T(8,128)(2,1)}) %all-gather.4.cloned.1.call-update) | async-done | bytes 1310736 | tf_op jit(solution)/shard_map/all_gather | solution.py:36
  172.4 0.0 all-gather.6.cloned.1.call-update
  172.4 0.9 multiply_subtract_fusion
  173.4 59.1 %all-gather.6.cloned.1.call-done = bf16[32,2,160,256]{3,2,1,0:T(8,128)(2,1)} async-done(((bf16[8,2,160,256]{3,2,1,0:T(8,128)(2,1)}), bf16[32,2,160,256]{3,2,1,0:T(8,128)(2,1)}) %all-gather.6.cloned.1.call-update) | async-done | bytes 5242896 | tf_op jit(solution)/shard_map/all_gather | solution.py:36
  232.5 2.9 %copy.56 = bf16[4,2,4,2,160,256]{5,4,3,2,1,0:T(8,128)(2,1)S(1)} copy(bf16[4,2,4,2,160,256]{5,4,3,1,0,2:T(8,128)(2,1)} %bitcast.24) | data formatting | bytes 10485760 | tf_op jit(solution)/shard_map/transpose | solution.py:40
  235.4 2.8 %copy.57 = bf16[2,32,160,256]{3,2,1,0:T(8,128)(2,1)} copy(bf16[2,32,160,256]{3,2,0,1:T(8,128)(2,1)S(1)} %bitcast.23) | data formatting | bytes 10485760 | tf_op jit(solution)/shard_map/transpose | solution.py:24
  (9 shorter events, 0.0 us)
Async XLA Ops:
  7.2 120.4 %copy-start = (s32[2,4]{1,0:T(2,128)S(1)}, s32[2,4]{1,0:T(2,128)}, u32[]{:S(2)}) copy-start(s32[2,4]{1,0:T(2,128)} %param.8) | copy-start | bytes 100
  8.5 16.3 %all-to-all-start = ((s32[32,1,1]{2,1,0:T(1,128)}), s32[32,1,1]{2,1,0:T(1,128)S(1)}, u32[]{:S(2)}, u32[]{:S(2)}) async-start(s32[32,1,1]{2,1,0:T(1,128)} %broadcast_in_dim.41), calls=%async_computation | async-start | bytes 32768 | tf_op jit(solution)/shard_map/all_to_all | solution.py:13
  25.4 14.7 %all-to-all-start.2 = ((f32[32,1,1]{2,1,0:T(1,128)}), f32[32,1,1]{2,1,0:T(1,128)S(1)}, u32[]{:S(2)}, u32[]{:S(2)}) async-start(f32[32,1,1]{2,1,0:T(1,128)} %broadcast_in_dim.43), calls=%async_computation.2 | async-start | bytes 32768 | tf_op jit(solution)/shard_map/all_to_all | solution.py:13
  40.1 71.1 %all-to-all-start.1 = ((bf16[1,2,5120,256]{3,1,0,2:T(2,128)(2,1)}), bf16[1,2,5120,256]{3,1,0,2:T(2,128)(2,1)}, u32[]{:S(2)}, u32[]{:S(2)}) async-start(bf16[1,2,5120,256]{3,1,0,2:T(2,128)(2,1)} %copy.53), calls=%async_computation.1 | async-start | bytes 10485760 | tf_op jit(solution)/shard_map/all_to_all | solution.py:51
  47.9 71.5 %copy-start.4 = (f32[2,160,256]{2,1,0:T(8,128)S(1)}, f32[2,160,256]{2,1,0:T(8,128)}, u32[]{:S(2)}) copy-start(f32[2,160,256]{2,1,0:T(8,128)} %param.10) | copy-start | bytes 983044
  47.9 71.5 %copy-start.5 = (f32[2,160,256]{2,1,0:T(8,128)S(1)}, f32[2,160,256]{2,1,0:T(8,128)}, u32[]{:S(2)}) copy-start(f32[2,160,256]{2,1,0:T(8,128)} %param.11) | copy-start | bytes 983044
  111.2 61.3 %copy-start.3 = (f32[2,160,256]{2,1,0:T(8,128)S(1)}, f32[2,160,256]{2,1,0:T(8,128)}, u32[]{:S(2)}) copy-start(f32[2,160,256]{2,1,0:T(8,128)} %param.9) | copy-start | bytes 983044
  120.3 115.0 %copy-start.1 = (f32[2,160,256]{2,1,0:T(8,128)}, f32[2,160,256]{2,1,0:T(8,128)S(1)}, u32[]{:S(2)}) copy-start(f32[2,160,256]{2,1,0:T(8,128)S(1)} %get-tuple-element.17) | copy-start | bytes 983044
  120.4 115.0 %copy-start.2 = (f32[2,160,256]{2,1,0:T(8,128)}, f32[2,160,256]{2,1,0:T(8,128)S(1)}, u32[]{:S(2)}) copy-start(f32[2,160,256]{2,1,0:T(8,128)S(1)} %get-tuple-element.18) | copy-start | bytes 983044
  121.4 17.0 %all-to-all-start.3 = ((bf16[4,2,160,256]{3,2,1,0:T(8,128)(2,1)}), bf16[4,2,160,256]{3,2,1,0:T(8,128)(2,1)S(1)}, u32[]{:S(2)}, u32[]{:S(2)}) async-start(bf16[4,2,160,256]{3,2,1,0:T(8,128)(2,1)} %broadcast_in_dim.45), calls=%async_computation.3 | async-start | bytes 1310720 | tf_op jit(solution)/shard_map/all_to_all | solution.py:13
  127.6 44.8 %all-gather.4.cloned.1.call-start = ((), (), s32[]{:S(2)}) async-start(), calls=%async_computation.4 | async-start | bytes 1638400 | tf_op jit(solution)/shard_map/all_gather | solution.py:36
  144.1 88.4 %all-gather.6.cloned.1.call-start = ((), (), s32[]{:S(2)}) async-start(), calls=%async_computation.5 | async-start | bytes 6553600 | tf_op jit(solution)/shard_map/all_gather | solution.py:36
Sparse Core Ops, SparseCore 0:
  144.2 28.1 all-gather.3
  174.1 58.3 all-gather.5
where the time goes:
time: 245 us
  waiting for transfers between devices  167 us (68%)
  starting transfers between devices  27.2 us (11%)
  local copies, waits for them, and re-layouts  18.9 us (8%)
  between operations  14.8 us (6%)
  other arithmetic  11.1 us (5%)
  blocking collectives  5.55 us (2%)
    all_gather x2, waiting for transfers between devices, all_blocks(): tiles = lax.all_gather(tiles, axes[k], axis=0, tiled=True)  87.4 us
    all_to_all x1, waiting for transfers between devices, local(): lax.all_to_all(partials, FSDP, split_axis=2, concat_axis=0, tiled=True)  62.3 us
    all_to_all x3, starting transfers between devices, sent_to_all(): lax.all_to_all(jnp.broadcast_to(value[None], (peers, *value.shape)), axis...  19.3 us
    all_to_all x3, waiting for transfers between devices, sent_to_all(): lax.all_to_all(jnp.broadcast_to(value[None], (peers, *value.shape)), axis...  17.6 us
    unnamed x13, local copies, waits for them, and re-layouts  10.9 us
    reduce_sum x1, other arithmetic, local(): jnp.sum(counts[:, None, None, None] * arrived.astype(jnp.float32), axis=0)  8.25 us
    all_to_all x1, starting transfers between devices, local(): lax.all_to_all(partials, FSDP, split_axis=2, concat_axis=0, tiled=True)  7.85 us
    all_gather x1, blocking collectives, all_blocks(): tiles = lax.all_gather(tiles, axes[k], axis=0, tiled=True)  5.55 us
  transfers between devices with their start and end apart: 6, of which 5 were waited for; matrix products, arithmetic and copies ran while one was open for 5% of the time, Pallas kernels for 0%

commit v1 on v0

--- a/solution.py
+++ b/solution.py
@@ -33,7 +33,9 @@
 def all_blocks(value, axes, order):
     tiles = value[None]
     for k in order:
-        tiles = lax.all_gather(tiles, axes[k], axis=0, tiled=True)
+        tiles = jnp.concatenate(
+            lax.all_to_all(jnp.stack([tiles] * lax.axis_size(axes[k])), axes[k], 0, 0), axis=0
+        )
     carried = [lax.axis_size(axes[k]) for k in reversed(order)]
     tiles = tiles.reshape(*carried, *value.shape)
     turned = sorted(range(len(order)), key=lambda place: order[len(order) - 1 - place])

time: 245 us -> 237 us (0.967); the launches traced: 245 us -> 233 us
  waiting for transfers between devices: 167 us -> 136 us
  blocking collectives: 5.55 us -> 28.8 us
  between operations: 14.8 us -> 1.44 us
  starting transfers between devices: 27.2 us -> 33.6 us
  local copies, waits for them, and re-layouts: 18.9 us -> 22.3 us
    all_gather x2 -> x0, waiting for transfers between devices: 87.4 us -> none  [all_blocks(): tiles = lax.all_gather(tiles, axes[k], axis=0, tiled=True)]
    all_to_all x0 -> x1, waiting for transfers between devices: none -> 55.8 us  [all_blocks(): lax.all_to_all(jnp.stack([tiles] * lax.axis_size(axes[k])), axes[k], 0, 0)]
    all_to_all x0 -> x2, blocking collectives: none -> 28.8 us  [all_blocks(): lax.all_to_all(jnp.stack([tiles] * lax.axis_size(axes[k])), axes[k], 0, 0)]
    all_to_all x0 -> x1, starting transfers between devices: none -> 6.52 us  [all_blocks(): lax.all_to_all(jnp.stack([tiles] * lax.axis_size(axes[k])), axes[k], 0, 0)]
    all_gather x1 -> x0, blocking collectives: 5.55 us -> none  [all_blocks(): tiles = lax.all_gather(tiles, axes[k], axis=0, tiled=True)]
    another operation x0 -> x4, local copies, waits for them, and re-layouts: none -> 3.23 us  [all_blocks(): jnp.stack([tiles] * lax.axis_size(axes[k]))]
    all_to_all x0 -> x2, local copies, waits for them, and re-layouts: none -> 3.03 us  [all_blocks(): lax.all_to_all(jnp.stack([tiles] * lax.axis_size(axes[k])), axes[k], 0, 0)]
    transpose x1 -> x0, local copies, waits for them, and re-layouts: 2.86 us -> none  [all_blocks(): tiles.transpose(*turned, *range(len(order), tiles.ndim))]
  transfers between devices with their start and end apart: 6 -> 5, of which waited for: 5 -> 4; matrix products, arithmetic and copies ran while one was open for 5% -> 6% of each run, Pallas kernels for 0% -> 0%
where the time goes in v1:
time: 237 us; the launch traced here: 233 us
  waiting for transfers between devices  136 us (57%)
  starting transfers between devices  33.6 us (14%)
  blocking collectives  28.8 us (12%)
  local copies, waits for them, and re-layouts  22.3 us (9%)
  other arithmetic  11.1 us (5%)
    all_to_all x1, waiting for transfers between devices, local(): lax.all_to_all(partials, FSDP, split_axis=2, concat_axis=0, tiled=True)  62.3 us
    all_to_all x1, waiting for transfers between devices, all_blocks(): lax.all_to_all(jnp.stack([tiles] * lax.axis_size(axes[k])), axes[k], 0, 0)  55.8 us
    all_to_all x2, blocking collectives, all_blocks(): lax.all_to_all(jnp.stack([tiles] * lax.axis_size(axes[k])), axes[k], 0, 0)  28.8 us
    all_to_all x3, starting transfers between devices, sent_to_all(): lax.all_to_all(jnp.broadcast_to(value[None], (peers, *value.shape)), axis...  19.3 us
    all_to_all x3, waiting for transfers between devices, sent_to_all(): lax.all_to_all(jnp.broadcast_to(value[None], (peers, *value.shape)), axis...  17.7 us
    unnamed x13, local copies, waits for them, and re-layouts  10.9 us
    reduce_sum x1, other arithmetic, local(): jnp.sum(counts[:, None, None, None] * arrived.astype(jnp.float32), axis=0)  8.22 us
    all_to_all x1, starting transfers between devices, local(): lax.all_to_all(partials, FSDP, split_axis=2, concat_axis=0, tiled=True)  7.85 us
  transfers between devices with their start and end apart: 5, of which 4 were waited for; matrix products, arithmetic and copies ran while one was open for 6% of the time, Pallas kernels for 0%

profile of v1, /device:TPU:1, one launch (start us, length us, event | category | flops | bytes accessed | tf_op | source)
XLA Modules:
  0.0 233.0 jit_solution(18400594791987795196)
XLA Ops:
  0.6 0.0 copy-start
  1.3 0.6 broadcast_in_dim.38
  1.9 9.2 %all-to-all-start = ((s32[32,1,1]{2,1,0:T(1,128)}), s32[32,1,1]{2,1,0:T(1,128)S(1)}, u32[]{:S(2)}, u32[]{:S(2)}) async-start(s32[32,1,1]{2,1,0:T(1,128)} %broadcast_in_dim.38), calls=%async_computation | async-start | bytes 32768 | tf_op jit(solution)/shard_map/all_to_all | solution.py:13
  11.1 7.1 %all-to-all-done = s32[32,1,1]{2,1,0:T(1,128)S(1)} async-done(((s32[32,1,1]{2,1,0:T(1,128)}), s32[32,1,1]{2,1,0:T(1,128)S(1)}, u32[]{:S(2)}, u32[]{:S(2)}) %all-to-all-start) | async-done | bytes 160 | tf_op jit(solution)/shard_map/all_to_all | solution.py:13
  18.2 0.6 broadcast_in_dim.40
  18.9 3.8 %all-to-all-start.2 = ((f32[32,1,1]{2,1,0:T(1,128)}), f32[32,1,1]{2,1,0:T(1,128)S(1)}, u32[]{:S(2)}, u32[]{:S(2)}) async-start(f32[32,1,1]{2,1,0:T(1,128)} %broadcast_in_dim.40), calls=%async_computation.2 | async-start | bytes 32768 | tf_op jit(solution)/shard_map/all_to_all | solution.py:13
  22.7 10.8 %copy.66 = bf16[1,2,5120,256]{3,1,0,2:T(2,128)(2,1)} copy(bf16[1,2,5120,256]{3,2,1,0:T(8,128)(2,1)} %param.6) | data formatting | bytes 10485760 | tf_op args[0]
  33.5 7.8 %all-to-all-start.1 = ((bf16[1,2,5120,256]{3,1,0,2:T(2,128)(2,1)}), bf16[1,2,5120,256]{3,1,0,2:T(2,128)(2,1)}, u32[]{:S(2)}, u32[]{:S(2)}) async-start(bf16[1,2,5120,256]{3,1,0,2:T(2,128)(2,1)} %copy.66), calls=%async_computation.1 | async-start | bytes 10485760 | tf_op jit(solution)/shard_map/all_to_all | solution.py:53
  41.4 0.0 copy-start.4
  41.4 0.0 copy-start.5
  41.4 0.6 reduce_sum.31
  42.0 0.3 convert_reduce_fusion
  42.4 62.3 %all-to-all-done.1 = bf16[1,2,5120,256]{3,1,0,2:T(2,128)(2,1)} async-done(((bf16[1,2,5120,256]{3,1,0,2:T(2,128)(2,1)}), bf16[1,2,5120,256]{3,1,0,2:T(2,128)(2,1)}, u32[]{:S(2)}, u32[]{:S(2)}) %all-to-all-start.1) | async-done | bytes 5242912 | tf_op jit(solution)/shard_map/all_to_all | solution.py:53
  104.6 8.2 %fusion = f32[2,160,256]{2,0,1:T(2,128)S(1)} fusion(bf16[1,2,32,160,256]{4,1,3,2,0:T(2,128)(2,1)} %bitcast.14, f32[32]{0:T(128)S(1)} %convert_reduce_fusion), kind=kLoop, calls=%fused_computation.1 | loop fusion | flops 7782400 | bytes 5570688 | tf_op jit(solution)/shard_map/reduce_sum | solution.py:54
  112.9 0.9 fusion.3
  113.8 0.0 copy-start.1
  113.8 1.0 broadcast_in_dim.42
  114.8 6.2 %all-to-all-start.3 = ((bf16[4,2,160,256]{3,2,1,0:T(8,128)(2,1)}), bf16[4,2,160,256]{3,2,1,0:T(8,128)(2,1)S(1)}, u32[]{:S(2)}, u32[]{:S(2)}) async-start(bf16[4,2,160,256]{3,2,1,0:T(8,128)(2,1)} %broadcast_in_dim.42), calls=%async_computation.3 | async-start | bytes 1310720 | tf_op jit(solution)/shard_map/all_to_all | solution.py:13
  121.0 0.2 dynamic-slice_reduce_fusion
  121.2 10.6 %all-to-all-done.3 = bf16[4,2,160,256]{3,2,1,0:T(8,128)(2,1)S(1)} async-done(((bf16[4,2,160,256]{3,2,1,0:T(8,128)(2,1)}), bf16[4,2,160,256]{3,2,1,0:T(8,128)(2,1)S(1)}, u32[]{:S(2)}, u32[]{:S(2)}) %all-to-all-start.3) | async-done | bytes 655392 | tf_op jit(solution)/shard_map/all_to_all | solution.py:13
  131.8 0.1 fusion.1
  131.9 7.1 %all_to_all.41 = bf16[2,1,2,160,256]{4,3,2,1,0:T(8,128)(2,1)S(1)} all-to-all(bf16[2,1,2,160,256]{4,3,2,1,0:T(8,128)(2,1)S(1)} %pad_maximum_fusion), channel_id=1, replica_groups=mesh['fsdp_0'=4,'fsdp_1'=2,'fsdp_2'=4,'tp'=4] {'fsdp_1'}, dimensions={0} | all-to-all | bytes 655360 | tf_op jit(solution)/shard_map/all_to_all | solution.py:37
  139.1 0.1 stack.10
  139.3 21.7 %all_to_all.42 = bf16[4,2,2,160,256]{4,3,1,2,0:T(8,128)(2,1)S(1)} all-to-all(bf16[4,2,2,160,256]{4,3,1,2,0:T(8,128)(2,1)S(1)} %stack.10), channel_id=1, replica_groups=mesh['fsdp_0'=4,'fsdp_1'=2,'fsdp_2'=4,'tp'=4] {'fsdp_0'}, dimensions={0} | all-to-all | bytes 2621440 | tf_op jit(solution)/shard_map/all_to_all | solution.py:37
  160.9 0.1 copy.70
  161.0 0.1 copy.71
  161.1 3.0 %stack.11 = bf16[4,8,2,160,256]{4,3,1,2,0:T(8,128)(2,1)} broadcast(bf16[8,2,160,256]{3,2,0,1:T(8,128)(2,1)S(1)} %copy.71), dimensions={1,2,3,4} | broadcast | bytes 6553600 | tf_op jit(solution)/shard_map/stack | solution.py:37
  164.1 6.5 %all-to-all-start.6 = ((bf16[4,8,2,160,256]{4,3,1,2,0:T(8,128)(2,1)}), bf16[4,8,2,160,256]{4,3,1,2,0:T(8,128)(2,1)}, u32[]{:S(2)}, u32[]{:S(2)}) async-start(bf16[4,8,2,160,256]{4,3,1,2,0:T(8,128)(2,1)} %stack.11), calls=%async_computation.6 | async-start | bytes 10485760 | tf_op jit(solution)/shard_map/all_to_all | solution.py:37
  170.6 0.9 multiply_subtract_fusion
  171.5 55.8 %all-to-all-done.6 = bf16[4,8,2,160,256]{4,3,1,2,0:T(8,128)(2,1)} async-done(((bf16[4,8,2,160,256]{4,3,1,2,0:T(8,128)(2,1)}), bf16[4,8,2,160,256]{4,3,1,2,0:T(8,128)(2,1)}, u32[]{:S(2)}, u32[]{:S(2)}) %all-to-all-start.6) | async-done | bytes 5242912 | tf_op jit(solution)/shard_map/all_to_all | solution.py:37
  227.3 2.9 %copy.72 = bf16[4,8,2,160,256]{4,3,2,0,1:T(8,128)(2,1)S(1)} copy(bf16[4,8,2,160,256]{4,3,1,2,0:T(8,128)(2,1)} %all-to-all-done.6) | data formatting | bytes 10485760 | tf_op jit(solution)/shard_map/all_to_all | solution.py:37
  230.3 2.8 %copy.73 = bf16[2,32,160,256]{3,2,1,0:T(8,128)(2,1)} copy(bf16[2,32,160,256]{3,2,0,1:T(8,128)(2,1)S(1)} %bitcast.26) | data formatting | bytes 10485760 | tf_op jit(solution)/shard_map/transpose | solution.py:24
  (12 shorter events, 0.1 us)
Async XLA Ops:
  0.6 120.4 %copy-start = (s32[2,4]{1,0:T(2,128)S(1)}, s32[2,4]{1,0:T(2,128)}, u32[]{:S(2)}) copy-start(s32[2,4]{1,0:T(2,128)} %param.8) | copy-start | bytes 100
  1.9 16.3 %all-to-all-start = ((s32[32,1,1]{2,1,0:T(1,128)}), s32[32,1,1]{2,1,0:T(1,128)S(1)}, u32[]{:S(2)}, u32[]{:S(2)}) async-start(s32[32,1,1]{2,1,0:T(1,128)} %broadcast_in_dim.38), calls=%async_computation | async-start | bytes 32768 | tf_op jit(solution)/shard_map/all_to_all | solution.py:13
  18.9 14.7 %all-to-all-start.2 = ((f32[32,1,1]{2,1,0:T(1,128)}), f32[32,1,1]{2,1,0:T(1,128)S(1)}, u32[]{:S(2)}, u32[]{:S(2)}) async-start(f32[32,1,1]{2,1,0:T(1,128)} %broadcast_in_dim.40), calls=%async_computation.2 | async-start | bytes 32768 | tf_op jit(solution)/shard_map/all_to_all | solution.py:13
  33.5 71.1 %all-to-all-start.1 = ((bf16[1,2,5120,256]{3,1,0,2:T(2,128)(2,1)}), bf16[1,2,5120,256]{3,1,0,2:T(2,128)(2,1)}, u32[]{:S(2)}, u32[]{:S(2)}) async-start(bf16[1,2,5120,256]{3,1,0,2:T(2,128)(2,1)} %copy.66), calls=%async_computation.1 | async-start | bytes 10485760 | tf_op jit(solution)/shard_map/all_to_all | solution.py:53
  41.4 71.5 %copy-start.4 = (f32[2,160,256]{2,1,0:T(8,128)S(1)}, f32[2,160,256]{2,1,0:T(8,128)}, u32[]{:S(2)}) copy-start(f32[2,160,256]{2,1,0:T(8,128)} %param.10) | copy-start | bytes 983044
  41.4 71.5 %copy-start.5 = (f32[2,160,256]{2,1,0:T(8,128)S(1)}, f32[2,160,256]{2,1,0:T(8,128)}, u32[]{:S(2)}) copy-start(f32[2,160,256]{2,1,0:T(8,128)} %param.11) | copy-start | bytes 983044
  113.8 56.9 %copy-start.1 = (f32[2,160,256]{2,1,0:T(8,128)}, f32[2,160,256]{2,1,0:T(8,128)S(1)}, u32[]{:S(2)}) copy-start(f32[2,160,256]{2,1,0:T(8,128)S(1)} %get-tuple-element.17) | copy-start | bytes 983044
  113.8 56.8 %copy-start.2 = (f32[2,160,256]{2,1,0:T(8,128)}, f32[2,160,256]{2,1,0:T(8,128)S(1)}, u32[]{:S(2)}) copy-start(f32[2,160,256]{2,1,0:T(8,128)S(1)} %get-tuple-element.18) | copy-start | bytes 983044
  114.8 17.0 %all-to-all-start.3 = ((bf16[4,2,160,256]{3,2,1,0:T(8,128)(2,1)}), bf16[4,2,160,256]{3,2,1,0:T(8,128)(2,1)S(1)}, u32[]{:S(2)}, u32[]{:S(2)}) async-start(bf16[4,2,160,256]{3,2,1,0:T(8,128)(2,1)} %broadcast_in_dim.42), calls=%async_computation.3 | async-start | bytes 1310720 | tf_op jit(solution)/shard_map/all_to_all | solution.py:13
  164.1 6.5 %copy-start.3 = (f32[2,160,256]{2,1,0:T(8,128)S(1)}, f32[2,160,256]{2,1,0:T(8,128)}, u32[]{:S(2)}) copy-start(f32[2,160,256]{2,1,0:T(8,128)} %param.9) | copy-start | bytes 983044
  164.1 63.2 %all-to-all-start.6 = ((bf16[4,8,2,160,256]{4,3,1,2,0:T(8,128)(2,1)}), bf16[4,8,2,160,256]{4,3,1,2,0:T(8,128)(2,1)}, u32[]{:S(2)}, u32[]{:S(2)}) async-start(bf16[4,8,2,160,256]{4,3,1,2,0:T(8,128)(2,1)} %stack.11), calls=%async_computation.6 | async-start | bytes 10485760 | tf_op jit(solution)/shard_map/all_to_all | solution.py:37
